TPU v7x, 32 devices: a whole 2x2x4 slice. The times are simulated.
32 devices in a mesh: data: 32 (over z, y, x, core).
Axes of the slice: x: 2, y: 2, z: 4, core: 2. Of those that a mesh axis runs over, the one named last changes fastest.
Arguments:
- feat_img: bfloat16 [32768, 768], P('data')
- feat_txt: bfloat16 [32768, 512], P('data')
- w_img: bfloat16 [768, 512], replicated
- w_txt: bfloat16 [512, 512], replicated
- log_temp: float32 [], replicated
- logit_bias: float32 [], replicated
- pair_ids: int32 [32768], P('data')
Outputs:
- output 1: float32 [], replicated
- output 2: float32 [], replicated
- output 3: float32 [], replicated
- output 4: float32 [768, 512], replicated
- output 5: float32 [512, 512], replicated
All inputs are finite; a program needn't handle non-finite values.
Results may differ from a plain program's by a relative error of at most 0.001.
Values are sent between devices in bfloat16 or wider.
A program may use at most 1 GiB of HBM per device.

v0:
```python
import jax
import jax.numpy as jnp
from jax import lax
from jax.sharding import PartitionSpec as P

CONTRACT_ROWS = (((0,), (0,)), ((), ()))
CONTRACT_COLS = (((1,), (1,)), ((), ()))


def embed_rows(feat_rows, weights):
    raw_emb = jnp.dot(feat_rows, weights, preferred_element_type=jnp.float32)
    inv_norm = lax.rsqrt(jnp.sum(raw_emb * raw_emb, axis=1, keepdims=True))
    unit_emb = raw_emb * inv_norm
    return unit_emb, inv_norm, unit_emb.astype(jnp.bfloat16)


def weight_grad(feat_rows, unit_emb, inv_norm, grad_emb):
    raw_grad = inv_norm * (grad_emb - unit_emb * jnp.sum(unit_emb * grad_emb, axis=1, keepdims=True))
    return lax.dot_general(feat_rows, raw_grad.astype(jnp.bfloat16), CONTRACT_ROWS, preferred_element_type=jnp.float32)


def tile_terms(emb_img, ids_img, emb_txt, ids_txt, temp_scale, logit_bias, total_rows):
    sim_tile = lax.dot_general(emb_img, emb_txt, CONTRACT_COLS, preferred_element_type=jnp.float32)
    label_sign = jnp.where(ids_img[:, None] == ids_txt[None, :], 1.0, -1.0).astype(jnp.float32)
    margin = -label_sign * (temp_scale * sim_tile + logit_bias)
    grad_tile = -label_sign * jax.nn.sigmoid(margin) / total_rows
    grad_bf = grad_tile.astype(jnp.bfloat16)
    part_img = jnp.dot(grad_bf, emb_txt, preferred_element_type=jnp.float32)
    part_txt = lax.dot_general(grad_bf, emb_img, CONTRACT_ROWS, preferred_element_type=jnp.float32)
    loss_part = jnp.sum(jax.nn.softplus(margin))
    return part_img, part_txt, loss_part, jnp.sum(grad_tile * sim_tile), jnp.sum(grad_tile)


def solution(mesh):
    n_dev = mesh.shape["data"]
    next_perm = [(src_dev, (src_dev + 1) % n_dev) for src_dev in range(n_dev)]

    def local_fn(feat_img, feat_txt, w_img, w_txt, log_temp, logit_bias, pair_ids):
        total_rows = feat_img.shape[0] * n_dev
        temp_scale = jnp.exp(log_temp)
        unit_img, inv_img, emb_img = embed_rows(feat_img, w_img)
        unit_txt, inv_txt, emb_txt = embed_rows(feat_txt, w_txt)

        def visit_block(hop_index, loop_state):
            txt_blk, ids_blk, acc_txt, acc_img, loss_sum, temp_sum, bias_sum = loop_state
            part_img, part_txt, loss_part, temp_part, bias_part = tile_terms(
                emb_img, pair_ids, txt_blk, ids_blk, temp_scale, logit_bias, total_rows)
            txt_blk, ids_blk, acc_txt = lax.ppermute((txt_blk, ids_blk, acc_txt + part_txt), "data", next_perm)
            return (txt_blk, ids_blk, acc_txt, acc_img + part_img,
                    loss_sum + loss_part, temp_sum + temp_part, bias_sum + bias_part)

        zero_rows = jnp.zeros(emb_img.shape, jnp.float32)
        zero_sum = jnp.zeros((), jnp.float32)
        loop_state = (emb_txt, pair_ids, zero_rows, zero_rows, zero_sum, zero_sum, zero_sum)
        loop_state = lax.fori_loop(0, n_dev - 1, visit_block, loop_state)
        txt_blk, ids_blk, acc_txt, acc_img, loss_sum, temp_sum, bias_sum = loop_state
        part_img, part_txt, loss_part, temp_part, bias_part = tile_terms(
            emb_img, pair_ids, txt_blk, ids_blk, temp_scale, logit_bias, total_rows)
        home_txt = lax.ppermute(acc_txt + part_txt, "data", next_perm)
        grad_img = temp_scale * (acc_img + part_img)
        grad_txt = temp_scale * home_txt
        dw_img = weight_grad(feat_img, unit_img, inv_img, grad_img)
        dw_txt = weight_grad(feat_txt, unit_txt, inv_txt, grad_txt)
        totals = lax.psum((loss_sum + loss_part, temp_sum + temp_part, bias_sum + bias_part, dw_img, dw_txt), "data")
        return totals[0] / total_rows, temp_scale * totals[1], totals[2], totals[3], totals[4]

    return jax.shard_map(
        local_fn,
        mesh=mesh,
        in_specs=(P("data", None), P("data", None), P(None, None), P(None, None), P(), P(), P("data")),
        out_specs=(P(), P(), P(), P(None, None), P(None, None)),
        check_vma=False,
    )
```

profile of v0, /device:TPU:0, one launch (start us, length us, event | category | flops | bytes accessed | tf_op | source)
XLA Modules:
  0.0 1934.7 jit_solution(11218561034182597685)
XLA Ops:
  23.4 1718.3 %while.23 = (s32[]{:T(128)}, bf16[1024,512]{1,0:T(8,128)(2,1)S(1)}, s32[1024]{0:T(1024)S(1)}, f32[1024,512]{1,0:T(8,128)}, f32[1024,512]{1,0:T(8,128)}, /*index=...) while((s32[]{:T(128)}, bf16[1024,512]{1,0:T(8,128)(2,1)S(1)}, ...), condition=%wide.region_6.7_spmd.clone, body=%wide.region_2.6_spmd.clone.sunk | while | flops 3245867008 | bytes 46170484 | solution.py:55
  48.0 31.9 %collective-permute-done.1 = s32[1024]{0:T(1024)S(1)} collective-permute-done((s32[1024]{0:T(1024)S(1)}, s32[1024]{0:T(1024)S(1)}, u32[]{:S(2)}, u32[]{:S(2)}) %collective-permute-start.1) | collective-permute-done | bytes 4128 | tf_op jit(solution)/shard_map/while/body/eval_jaxpr/ppermute | solution.py:48
  102.1 33.2 %collective-permute-done.1 = s32[1024]{0:T(1024)S(1)} collective-permute-done((s32[1024]{0:T(1024)S(1)}, s32[1024]{0:T(1024)S(1)}, u32[]{:S(2)}, u32[]{:S(2)}) %collective-permute-start.1) | collective-permute-done | bytes 4128 | tf_op jit(solution)/shard_map/while/body/eval_jaxpr/ppermute | solution.py:48
  136.9 8.5 fusion.44
  157.5 33.2 %collective-permute-done.1 = s32[1024]{0:T(1024)S(1)} collective-permute-done((s32[1024]{0:T(1024)S(1)}, s32[1024]{0:T(1024)S(1)}, u32[]{:S(2)}, u32[]{:S(2)}) %collective-permute-start.1) | collective-permute-done | bytes 4128 | tf_op jit(solution)/shard_map/while/body/eval_jaxpr/ppermute | solution.py:48
  192.3 8.5 fusion.44
  212.9 33.2 %collective-permute-done.1 = s32[1024]{0:T(1024)S(1)} collective-permute-done((s32[1024]{0:T(1024)S(1)}, s32[1024]{0:T(1024)S(1)}, u32[]{:S(2)}, u32[]{:S(2)}) %collective-permute-start.1) | collective-permute-done | bytes 4128 | tf_op jit(solution)/shard_map/while/body/eval_jaxpr/ppermute | solution.py:48
  268.3 33.2 %collective-permute-done.1 = s32[1024]{0:T(1024)S(1)} collective-permute-done((s32[1024]{0:T(1024)S(1)}, s32[1024]{0:T(1024)S(1)}, u32[]{:S(2)}, u32[]{:S(2)}) %collective-permute-start.1) | collective-permute-done | bytes 4128 | tf_op jit(solution)/shard_map/while/body/eval_jaxpr/ppermute | solution.py:48
  323.7 33.2 %collective-permute-done.1 = s32[1024]{0:T(1024)S(1)} collective-permute-done((s32[1024]{0:T(1024)S(1)}, s32[1024]{0:T(1024)S(1)}, u32[]{:S(2)}, u32[]{:S(2)}) %collective-permute-start.1) | collective-permute-done | bytes 4128 | tf_op jit(solution)/shard_map/while/body/eval_jaxpr/ppermute | solution.py:48
  358.4 8.5 fusion.44
  379.0 33.2 %collective-permute-done.1 = s32[1024]{0:T(1024)S(1)} collective-permute-done((s32[1024]{0:T(1024)S(1)}, s32[1024]{0:T(1024)S(1)}, u32[]{:S(2)}, u32[]{:S(2)}) %collective-permute-start.1) | collective-permute-done | bytes 4128 | tf_op jit(solution)/shard_map/while/body/eval_jaxpr/ppermute | solution.py:48
  413.8 8.5 fusion.44
  434.4 33.2 %collective-permute-done.1 = s32[1024]{0:T(1024)S(1)} collective-permute-done((s32[1024]{0:T(1024)S(1)}, s32[1024]{0:T(1024)S(1)}, u32[]{:S(2)}, u32[]{:S(2)}) %collective-permute-start.1) | collective-permute-done | bytes 4128 | tf_op jit(solution)/shard_map/while/body/eval_jaxpr/ppermute | solution.py:48
  469.2 8.5 fusion.44
  489.8 33.2 %collective-permute-done.1 = s32[1024]{0:T(1024)S(1)} collective-permute-done((s32[1024]{0:T(1024)S(1)}, s32[1024]{0:T(1024)S(1)}, u32[]{:S(2)}, u32[]{:S(2)}) %collective-permute-start.1) | collective-permute-done | bytes 4128 | tf_op jit(solution)/shard_map/while/body/eval_jaxpr/ppermute | solution.py:48
  545.2 33.2 %collective-permute-done.1 = s32[1024]{0:T(1024)S(1)} collective-permute-done((s32[1024]{0:T(1024)S(1)}, s32[1024]{0:T(1024)S(1)}, u32[]{:S(2)}, u32[]{:S(2)}) %collective-permute-start.1) | collective-permute-done | bytes 4128 | tf_op jit(solution)/shard_map/while/body/eval_jaxpr/ppermute | solution.py:48
  600.6 33.2 %collective-permute-done.1 = s32[1024]{0:T(1024)S(1)} collective-permute-done((s32[1024]{0:T(1024)S(1)}, s32[1024]{0:T(1024)S(1)}, u32[]{:S(2)}, u32[]{:S(2)}) %collective-permute-start.1) | collective-permute-done | bytes 4128 | tf_op jit(solution)/shard_map/while/body/eval_jaxpr/ppermute | solution.py:48
  635.4 8.5 fusion.44
  656.0 33.2 %collective-permute-done.1 = s32[1024]{0:T(1024)S(1)} collective-permute-done((s32[1024]{0:T(1024)S(1)}, s32[1024]{0:T(1024)S(1)}, u32[]{:S(2)}, u32[]{:S(2)}) %collective-permute-start.1) | collective-permute-done | bytes 4128 | tf_op jit(solution)/shard_map/while/body/eval_jaxpr/ppermute | solution.py:48
  690.8 8.5 fusion.44
  711.4 33.2 %collective-permute-done.1 = s32[1024]{0:T(1024)S(1)} collective-permute-done((s32[1024]{0:T(1024)S(1)}, s32[1024]{0:T(1024)S(1)}, u32[]{:S(2)}, u32[]{:S(2)}) %collective-permute-start.1) | collective-permute-done | bytes 4128 | tf_op jit(solution)/shard_map/while/body/eval_jaxpr/ppermute | solution.py:48
  746.2 8.5 fusion.44
  766.8 33.2 %collective-permute-done.1 = s32[1024]{0:T(1024)S(1)} collective-permute-done((s32[1024]{0:T(1024)S(1)}, s32[1024]{0:T(1024)S(1)}, u32[]{:S(2)}, u32[]{:S(2)}) %collective-permute-start.1) | collective-permute-done | bytes 4128 | tf_op jit(solution)/shard_map/while/body/eval_jaxpr/ppermute | solution.py:48
  822.2 33.2 %collective-permute-done.1 = s32[1024]{0:T(1024)S(1)} collective-permute-done((s32[1024]{0:T(1024)S(1)}, s32[1024]{0:T(1024)S(1)}, u32[]{:S(2)}, u32[]{:S(2)}) %collective-permute-start.1) | collective-permute-done | bytes 4128 | tf_op jit(solution)/shard_map/while/body/eval_jaxpr/ppermute | solution.py:48
  857.0 8.5 fusion.44
  877.6 33.2 %collective-permute-done.1 = s32[1024]{0:T(1024)S(1)} collective-permute-done((s32[1024]{0:T(1024)S(1)}, s32[1024]{0:T(1024)S(1)}, u32[]{:S(2)}, u32[]{:S(2)}) %collective-permute-start.1) | collective-permute-done | bytes 4128 | tf_op jit(solution)/shard_map/while/body/eval_jaxpr/ppermute | solution.py:48
  912.4 8.5 fusion.44
  933.0 33.2 %collective-permute-done.1 = s32[1024]{0:T(1024)S(1)} collective-permute-done((s32[1024]{0:T(1024)S(1)}, s32[1024]{0:T(1024)S(1)}, u32[]{:S(2)}, u32[]{:S(2)}) %collective-permute-start.1) | collective-permute-done | bytes 4128 | tf_op jit(solution)/shard_map/while/body/eval_jaxpr/ppermute | solution.py:48
  967.8 8.5 fusion.44
  988.4 33.2 %collective-permute-done.1 = s32[1024]{0:T(1024)S(1)} collective-permute-done((s32[1024]{0:T(1024)S(1)}, s32[1024]{0:T(1024)S(1)}, u32[]{:S(2)}, u32[]{:S(2)}) %collective-permute-start.1) | collective-permute-done | bytes 4128 | tf_op jit(solution)/shard_map/while/body/eval_jaxpr/ppermute | solution.py:48
  1043.8 33.2 %collective-permute-done.1 = s32[1024]{0:T(1024)S(1)} collective-permute-done((s32[1024]{0:T(1024)S(1)}, s32[1024]{0:T(1024)S(1)}, u32[]{:S(2)}, u32[]{:S(2)}) %collective-permute-start.1) | collective-permute-done | bytes 4128 | tf_op jit(solution)/shard_map/while/body/eval_jaxpr/ppermute | solution.py:48
  1099.2 33.2 %collective-permute-done.1 = s32[1024]{0:T(1024)S(1)} collective-permute-done((s32[1024]{0:T(1024)S(1)}, s32[1024]{0:T(1024)S(1)}, u32[]{:S(2)}, u32[]{:S(2)}) %collective-permute-start.1) | collective-permute-done | bytes 4128 | tf_op jit(solution)/shard_map/while/body/eval_jaxpr/ppermute | solution.py:48
  1134.0 8.5 fusion.44
  1154.6 33.2 %collective-permute-done.1 = s32[1024]{0:T(1024)S(1)} collective-permute-done((s32[1024]{0:T(1024)S(1)}, s32[1024]{0:T(1024)S(1)}, u32[]{:S(2)}, u32[]{:S(2)}) %collective-permute-start.1) | collective-permute-done | bytes 4128 | tf_op jit(solution)/shard_map/while/body/eval_jaxpr/ppermute | solution.py:48
  1189.4 8.5 fusion.44
  1210.0 33.2 %collective-permute-done.1 = s32[1024]{0:T(1024)S(1)} collective-permute-done((s32[1024]{0:T(1024)S(1)}, s32[1024]{0:T(1024)S(1)}, u32[]{:S(2)}, u32[]{:S(2)}) %collective-permute-start.1) | collective-permute-done | bytes 4128 | tf_op jit(solution)/shard_map/while/body/eval_jaxpr/ppermute | solution.py:48
  1265.3 33.2 %collective-permute-done.1 = s32[1024]{0:T(1024)S(1)} collective-permute-done((s32[1024]{0:T(1024)S(1)}, s32[1024]{0:T(1024)S(1)}, u32[]{:S(2)}, u32[]{:S(2)}) %collective-permute-start.1) | collective-permute-done | bytes 4128 | tf_op jit(solution)/shard_map/while/body/eval_jaxpr/ppermute | solution.py:48
  1320.7 33.2 %collective-permute-done.1 = s32[1024]{0:T(1024)S(1)} collective-permute-done((s32[1024]{0:T(1024)S(1)}, s32[1024]{0:T(1024)S(1)}, u32[]{:S(2)}, u32[]{:S(2)}) %collective-permute-start.1) | collective-permute-done | bytes 4128 | tf_op jit(solution)/shard_map/while/body/eval_jaxpr/ppermute | solution.py:48
  1376.1 33.2 %collective-permute-done.1 = s32[1024]{0:T(1024)S(1)} collective-permute-done((s32[1024]{0:T(1024)S(1)}, s32[1024]{0:T(1024)S(1)}, u32[]{:S(2)}, u32[]{:S(2)}) %collective-permute-start.1) | collective-permute-done | bytes 4128 | tf_op jit(solution)/shard_map/while/body/eval_jaxpr/ppermute | solution.py:48
  1431.5 33.2 %collective-permute-done.1 = s32[1024]{0:T(1024)S(1)} collective-permute-done((s32[1024]{0:T(1024)S(1)}, s32[1024]{0:T(1024)S(1)}, u32[]{:S(2)}, u32[]{:S(2)}) %collective-permute-start.1) | collective-permute-done | bytes 4128 | tf_op jit(solution)/shard_map/while/body/eval_jaxpr/ppermute | solution.py:48
  1486.9 33.2 %collective-permute-done.1 = s32[1024]{0:T(1024)S(1)} collective-permute-done((s32[1024]{0:T(1024)S(1)}, s32[1024]{0:T(1024)S(1)}, u32[]{:S(2)}, u32[]{:S(2)}) %collective-permute-start.1) | collective-permute-done | bytes 4128 | tf_op jit(solution)/shard_map/while/body/eval_jaxpr/ppermute | solution.py:48
  1542.3 33.2 %collective-permute-done.1 = s32[1024]{0:T(1024)S(1)} collective-permute-done((s32[1024]{0:T(1024)S(1)}, s32[1024]{0:T(1024)S(1)}, u32[]{:S(2)}, u32[]{:S(2)}) %collective-permute-start.1) | collective-permute-done | bytes 4128 | tf_op jit(solution)/shard_map/while/body/eval_jaxpr/ppermute | solution.py:48
  1597.7 33.2 %collective-permute-done.1 = s32[1024]{0:T(1024)S(1)} collective-permute-done((s32[1024]{0:T(1024)S(1)}, s32[1024]{0:T(1024)S(1)}, u32[]{:S(2)}, u32[]{:S(2)}) %collective-permute-start.1) | collective-permute-done | bytes 4128 | tf_op jit(solution)/shard_map/while/body/eval_jaxpr/ppermute | solution.py:48
  1653.1 33.2 %collective-permute-done.1 = s32[1024]{0:T(1024)S(1)} collective-permute-done((s32[1024]{0:T(1024)S(1)}, s32[1024]{0:T(1024)S(1)}, u32[]{:S(2)}, u32[]{:S(2)}) %collective-permute-start.1) | collective-permute-done | bytes 4128 | tf_op jit(solution)/shard_map/while/body/eval_jaxpr/ppermute | solution.py:48
  1708.5 33.2 %collective-permute-done.1 = s32[1024]{0:T(1024)S(1)} collective-permute-done((s32[1024]{0:T(1024)S(1)}, s32[1024]{0:T(1024)S(1)}, u32[]{:S(2)}, u32[]{:S(2)}) %collective-permute-start.1) | collective-permute-done | bytes 4128 | tf_op jit(solution)/shard_map/while/body/eval_jaxpr/ppermute | solution.py:48
  1764.1 19.5 %collective-permute-done.3 = f32[1024,512]{0,1:T(8,128)} collective-permute-done((f32[1024,512]{0,1:T(8,128)}, f32[1024,512]{0,1:T(8,128)}, u32[]{:S(2)}, u32[]{:S(2)}) %collective-permute-start.3) | collective-permute-done | bytes 2097184 | tf_op jit(solution)/shard_map/ppermute | solution.py:59
  1790.9 37.2 %all-reduce = (f32[]{:T(128)}, f32[]{:T(128)}, f32[]{:T(128)}) all-reduce(f32[]{:T(128)S(6)} %add.71, f32[]{:T(128)S(6)} %add.73, f32[]{:T(128)S(6)} %add.74), channel_id=1, replica_groups=mesh['data'=32] {'data'}, use_global_device_ids=true, to_apply=%region_8.9 | all-reduce | flops 3 | bytes 24 | tf_op jit(solution)/shard_map/psum | solution.py:64
  1829.5 91.7 %all-reduce.4.cloned.1.call-done = (f32[768,512]{0,1:T(8,128)}, f32[512,512]{0,1:T(8,128)}) async-done(((f32[768,512]{0,1:T(8,128)}, f32[512,512]{0,1:T(8,128)}), (f32[768,512]{0,1:T(8,128)}, f32[512,512]{0,1:T(8,128)})) %all-reduce.4.cloned.1.call-update) | async-done | bytes 2621456 | tf_op jit(solution)/shard_map/psum | solution.py:64
  (479 shorter events, 566.4 us)
Async XLA Ops:
  7.2 1913.9 %all-reduce.4.cloned.1.call-start = ((), (), s32[]{:S(2)}) async-start(), calls=%async_computation | async-start | bytes 5242880 | tf_op jit(solution)/shard_map/psum | solution.py:64
  38.4 41.4 %collective-permute-start.2 = (f32[1024,512]{1,0:T(8,128)}, f32[1024,512]{1,0:T(8,128)}, u32[]{:S(2)}, u32[]{:S(2)}) collective-permute-start(f32[1024,512]{1,0:T(8,128)} %convolution_add_fusion.3), channel_id=1, source_target_pairs={{0,1},{1,2},{2,3},{3,4},{4,5},{5,6},{6,7},{7,8},{8,9},{9,10},{10,1... | collective-permute-start | bytes 6291464 | tf_op jit(solution)/shard_map/while/body/eval_jaxpr/ppermute | solution.py:48
  39.0 40.9 %collective-permute-start = (bf16[1024,512]{1,0:T(8,128)(2,1)}, bf16[1024,512]{1,0:T(8,128)(2,1)S(1)}, u32[]{:S(2)}, u32[]{:S(2)}) collective-permute-start(bf16[1024,512]{1,0:T(8,128)(2,1)} %copy.29), channel_id=1, source_target_pairs={{0,1},{1,2},{2,3},{3,4},{4,5},{5,6},{6,7},{7,8},{8,9},{9,10},{10,1... | collective-permute-start | bytes 3145736 | tf_op jit(solution)/shard_map/while/body/eval_jaxpr/ppermute | solution.py:48
  94.9 40.3 %collective-permute-start.2 = (f32[1024,512]{1,0:T(8,128)}, f32[1024,512]{1,0:T(8,128)}, u32[]{:S(2)}, u32[]{:S(2)}) collective-permute-start(f32[1024,512]{1,0:T(8,128)} %convolution_add_fusion.3), channel_id=1, source_target_pairs={{0,1},{1,2},{2,3},{3,4},{4,5},{5,6},{6,7},{7,8},{8,9},{9,10},{10,1... | collective-permute-start | bytes 6291464 | tf_op jit(solution)/shard_map/while/body/eval_jaxpr/ppermute | solution.py:48
  94.9 40.3 %collective-permute-start = (bf16[1024,512]{1,0:T(8,128)(2,1)}, bf16[1024,512]{1,0:T(8,128)(2,1)S(1)}, u32[]{:S(2)}, u32[]{:S(2)}) collective-permute-start(bf16[1024,512]{1,0:T(8,128)(2,1)} %copy.29), channel_id=1, source_target_pairs={{0,1},{1,2},{2,3},{3,4},{4,5},{5,6},{6,7},{7,8},{8,9},{9,10},{10,1... | collective-permute-start | bytes 3145736 | tf_op jit(solution)/shard_map/while/body/eval_jaxpr/ppermute | solution.py:48
  150.3 40.3 %collective-permute-start.2 = (f32[1024,512]{1,0:T(8,128)}, f32[1024,512]{1,0:T(8,128)}, u32[]{:S(2)}, u32[]{:S(2)}) collective-permute-start(f32[1024,512]{1,0:T(8,128)} %convolution_add_fusion.3), channel_id=1, source_target_pairs={{0,1},{1,2},{2,3},{3,4},{4,5},{5,6},{6,7},{7,8},{8,9},{9,10},{10,1... | collective-permute-start | bytes 6291464 | tf_op jit(solution)/shard_map/while/body/eval_jaxpr/ppermute | solution.py:48
  150.3 40.3 %collective-permute-start = (bf16[1024,512]{1,0:T(8,128)(2,1)}, bf16[1024,512]{1,0:T(8,128)(2,1)S(1)}, u32[]{:S(2)}, u32[]{:S(2)}) collective-permute-start(bf16[1024,512]{1,0:T(8,128)(2,1)} %copy.29), channel_id=1, source_target_pairs={{0,1},{1,2},{2,3},{3,4},{4,5},{5,6},{6,7},{7,8},{8,9},{9,10},{10,1... | collective-permute-start | bytes 3145736 | tf_op jit(solution)/shard_map/while/body/eval_jaxpr/ppermute | solution.py:48
  205.7 40.3 %collective-permute-start.2 = (f32[1024,512]{1,0:T(8,128)}, f32[1024,512]{1,0:T(8,128)}, u32[]{:S(2)}, u32[]{:S(2)}) collective-permute-start(f32[1024,512]{1,0:T(8,128)} %convolution_add_fusion.3), channel_id=1, source_target_pairs={{0,1},{1,2},{2,3},{3,4},{4,5},{5,6},{6,7},{7,8},{8,9},{9,10},{10,1... | collective-permute-start | bytes 6291464 | tf_op jit(solution)/shard_map/while/body/eval_jaxpr/ppermute | solution.py:48
  205.7 40.3 %collective-permute-start = (bf16[1024,512]{1,0:T(8,128)(2,1)}, bf16[1024,512]{1,0:T(8,128)(2,1)S(1)}, u32[]{:S(2)}, u32[]{:S(2)}) collective-permute-start(bf16[1024,512]{1,0:T(8,128)(2,1)} %copy.29), channel_id=1, source_target_pairs={{0,1},{1,2},{2,3},{3,4},{4,5},{5,6},{6,7},{7,8},{8,9},{9,10},{10,1... | collective-permute-start | bytes 3145736 | tf_op jit(solution)/shard_map/while/body/eval_jaxpr/ppermute | solution.py:48
  261.1 40.3 %collective-permute-start.2 = (f32[1024,512]{1,0:T(8,128)}, f32[1024,512]{1,0:T(8,128)}, u32[]{:S(2)}, u32[]{:S(2)}) collective-permute-start(f32[1024,512]{1,0:T(8,128)} %convolution_add_fusion.3), channel_id=1, source_target_pairs={{0,1},{1,2},{2,3},{3,4},{4,5},{5,6},{6,7},{7,8},{8,9},{9,10},{10,1... | collective-permute-start | bytes 6291464 | tf_op jit(solution)/shard_map/while/body/eval_jaxpr/ppermute | solution.py:48
  261.1 40.3 %collective-permute-start = (bf16[1024,512]{1,0:T(8,128)(2,1)}, bf16[1024,512]{1,0:T(8,128)(2,1)S(1)}, u32[]{:S(2)}, u32[]{:S(2)}) collective-permute-start(bf16[1024,512]{1,0:T(8,128)(2,1)} %copy.29), channel_id=1, source_target_pairs={{0,1},{1,2},{2,3},{3,4},{4,5},{5,6},{6,7},{7,8},{8,9},{9,10},{10,1... | collective-permute-start | bytes 3145736 | tf_op jit(solution)/shard_map/while/body/eval_jaxpr/ppermute | solution.py:48
  316.5 40.3 %collective-permute-start.2 = (f32[1024,512]{1,0:T(8,128)}, f32[1024,512]{1,0:T(8,128)}, u32[]{:S(2)}, u32[]{:S(2)}) collective-permute-start(f32[1024,512]{1,0:T(8,128)} %convolution_add_fusion.3), channel_id=1, source_target_pairs={{0,1},{1,2},{2,3},{3,4},{4,5},{5,6},{6,7},{7,8},{8,9},{9,10},{10,1... | collective-permute-start | bytes 6291464 | tf_op jit(solution)/shard_map/while/body/eval_jaxpr/ppermute | solution.py:48
  316.5 40.3 %collective-permute-start = (bf16[1024,512]{1,0:T(8,128)(2,1)}, bf16[1024,512]{1,0:T(8,128)(2,1)S(1)}, u32[]{:S(2)}, u32[]{:S(2)}) collective-permute-start(bf16[1024,512]{1,0:T(8,128)(2,1)} %copy.29), channel_id=1, source_target_pairs={{0,1},{1,2},{2,3},{3,4},{4,5},{5,6},{6,7},{7,8},{8,9},{9,10},{10,1... | collective-permute-start | bytes 3145736 | tf_op jit(solution)/shard_map/while/body/eval_jaxpr/ppermute | solution.py:48
  371.9 40.3 %collective-permute-start.2 = (f32[1024,512]{1,0:T(8,128)}, f32[1024,512]{1,0:T(8,128)}, u32[]{:S(2)}, u32[]{:S(2)}) collective-permute-start(f32[1024,512]{1,0:T(8,128)} %convolution_add_fusion.3), channel_id=1, source_target_pairs={{0,1},{1,2},{2,3},{3,4},{4,5},{5,6},{6,7},{7,8},{8,9},{9,10},{10,1... | collective-permute-start | bytes 6291464 | tf_op jit(solution)/shard_map/while/body/eval_jaxpr/ppermute | solution.py:48
  371.9 40.3 %collective-permute-start = (bf16[1024,512]{1,0:T(8,128)(2,1)}, bf16[1024,512]{1,0:T(8,128)(2,1)S(1)}, u32[]{:S(2)}, u32[]{:S(2)}) collective-permute-start(bf16[1024,512]{1,0:T(8,128)(2,1)} %copy.29), channel_id=1, source_target_pairs={{0,1},{1,2},{2,3},{3,4},{4,5},{5,6},{6,7},{7,8},{8,9},{9,10},{10,1... | collective-permute-start | bytes 3145736 | tf_op jit(solution)/shard_map/while/body/eval_jaxpr/ppermute | solution.py:48
  427.3 40.3 %collective-permute-start.2 = (f32[1024,512]{1,0:T(8,128)}, f32[1024,512]{1,0:T(8,128)}, u32[]{:S(2)}, u32[]{:S(2)}) collective-permute-start(f32[1024,512]{1,0:T(8,128)} %convolution_add_fusion.3), channel_id=1, source_target_pairs={{0,1},{1,2},{2,3},{3,4},{4,5},{5,6},{6,7},{7,8},{8,9},{9,10},{10,1... | collective-permute-start | bytes 6291464 | tf_op jit(solution)/shard_map/while/body/eval_jaxpr/ppermute | solution.py:48
  427.3 40.3 %collective-permute-start = (bf16[1024,512]{1,0:T(8,128)(2,1)}, bf16[1024,512]{1,0:T(8,128)(2,1)S(1)}, u32[]{:S(2)}, u32[]{:S(2)}) collective-permute-start(bf16[1024,512]{1,0:T(8,128)(2,1)} %copy.29), channel_id=1, source_target_pairs={{0,1},{1,2},{2,3},{3,4},{4,5},{5,6},{6,7},{7,8},{8,9},{9,10},{10,1... | collective-permute-start | bytes 3145736 | tf_op jit(solution)/shard_map/while/body/eval_jaxpr/ppermute | solution.py:48
  482.7 40.3 %collective-permute-start.2 = (f32[1024,512]{1,0:T(8,128)}, f32[1024,512]{1,0:T(8,128)}, u32[]{:S(2)}, u32[]{:S(2)}) collective-permute-start(f32[1024,512]{1,0:T(8,128)} %convolution_add_fusion.3), channel_id=1, source_target_pairs={{0,1},{1,2},{2,3},{3,4},{4,5},{5,6},{6,7},{7,8},{8,9},{9,10},{10,1... | collective-permute-start | bytes 6291464 | tf_op jit(solution)/shard_map/while/body/eval_jaxpr/ppermute | solution.py:48
  482.7 40.3 %collective-permute-start = (bf16[1024,512]{1,0:T(8,128)(2,1)}, bf16[1024,512]{1,0:T(8,128)(2,1)S(1)}, u32[]{:S(2)}, u32[]{:S(2)}) collective-permute-start(bf16[1024,512]{1,0:T(8,128)(2,1)} %copy.29), channel_id=1, source_target_pairs={{0,1},{1,2},{2,3},{3,4},{4,5},{5,6},{6,7},{7,8},{8,9},{9,10},{10,1... | collective-permute-start | bytes 3145736 | tf_op jit(solution)/shard_map/while/body/eval_jaxpr/ppermute | solution.py:48
  538.1 40.3 %collective-permute-start.2 = (f32[1024,512]{1,0:T(8,128)}, f32[1024,512]{1,0:T(8,128)}, u32[]{:S(2)}, u32[]{:S(2)}) collective-permute-start(f32[1024,512]{1,0:T(8,128)} %convolution_add_fusion.3), channel_id=1, source_target_pairs={{0,1},{1,2},{2,3},{3,4},{4,5},{5,6},{6,7},{7,8},{8,9},{9,10},{10,1... | collective-permute-start | bytes 6291464 | tf_op jit(solution)/shard_map/while/body/eval_jaxpr/ppermute | solution.py:48
  538.1 40.3 %collective-permute-start = (bf16[1024,512]{1,0:T(8,128)(2,1)}, bf16[1024,512]{1,0:T(8,128)(2,1)S(1)}, u32[]{:S(2)}, u32[]{:S(2)}) collective-permute-start(bf16[1024,512]{1,0:T(8,128)(2,1)} %copy.29), channel_id=1, source_target_pairs={{0,1},{1,2},{2,3},{3,4},{4,5},{5,6},{6,7},{7,8},{8,9},{9,10},{10,1... | collective-permute-start | bytes 3145736 | tf_op jit(solution)/shard_map/while/body/eval_jaxpr/ppermute | solution.py:48
  593.5 40.3 %collective-permute-start.2 = (f32[1024,512]{1,0:T(8,128)}, f32[1024,512]{1,0:T(8,128)}, u32[]{:S(2)}, u32[]{:S(2)}) collective-permute-start(f32[1024,512]{1,0:T(8,128)} %convolution_add_fusion.3), channel_id=1, source_target_pairs={{0,1},{1,2},{2,3},{3,4},{4,5},{5,6},{6,7},{7,8},{8,9},{9,10},{10,1... | collective-permute-start | bytes 6291464 | tf_op jit(solution)/shard_map/while/body/eval_jaxpr/ppermute | solution.py:48
  593.5 40.3 %collective-permute-start = (bf16[1024,512]{1,0:T(8,128)(2,1)}, bf16[1024,512]{1,0:T(8,128)(2,1)S(1)}, u32[]{:S(2)}, u32[]{:S(2)}) collective-permute-start(bf16[1024,512]{1,0:T(8,128)(2,1)} %copy.29), channel_id=1, source_target_pairs={{0,1},{1,2},{2,3},{3,4},{4,5},{5,6},{6,7},{7,8},{8,9},{9,10},{10,1... | collective-permute-start | bytes 3145736 | tf_op jit(solution)/shard_map/while/body/eval_jaxpr/ppermute | solution.py:48
  648.9 40.3 %collective-permute-start.2 = (f32[1024,512]{1,0:T(8,128)}, f32[1024,512]{1,0:T(8,128)}, u32[]{:S(2)}, u32[]{:S(2)}) collective-permute-start(f32[1024,512]{1,0:T(8,128)} %convolution_add_fusion.3), channel_id=1, source_target_pairs={{0,1},{1,2},{2,3},{3,4},{4,5},{5,6},{6,7},{7,8},{8,9},{9,10},{10,1... | collective-permute-start | bytes 6291464 | tf_op jit(solution)/shard_map/while/body/eval_jaxpr/ppermute | solution.py:48
  648.9 40.3 %collective-permute-start = (bf16[1024,512]{1,0:T(8,128)(2,1)}, bf16[1024,512]{1,0:T(8,128)(2,1)S(1)}, u32[]{:S(2)}, u32[]{:S(2)}) collective-permute-start(bf16[1024,512]{1,0:T(8,128)(2,1)} %copy.29), channel_id=1, source_target_pairs={{0,1},{1,2},{2,3},{3,4},{4,5},{5,6},{6,7},{7,8},{8,9},{9,10},{10,1... | collective-permute-start | bytes 3145736 | tf_op jit(solution)/shard_map/while/body/eval_jaxpr/ppermute | solution.py:48
  704.3 40.3 %collective-permute-start.2 = (f32[1024,512]{1,0:T(8,128)}, f32[1024,512]{1,0:T(8,128)}, u32[]{:S(2)}, u32[]{:S(2)}) collective-permute-start(f32[1024,512]{1,0:T(8,128)} %convolution_add_fusion.3), channel_id=1, source_target_pairs={{0,1},{1,2},{2,3},{3,4},{4,5},{5,6},{6,7},{7,8},{8,9},{9,10},{10,1... | collective-permute-start | bytes 6291464 | tf_op jit(solution)/shard_map/while/body/eval_jaxpr/ppermute | solution.py:48
  704.3 40.3 %collective-permute-start = (bf16[1024,512]{1,0:T(8,128)(2,1)}, bf16[1024,512]{1,0:T(8,128)(2,1)S(1)}, u32[]{:S(2)}, u32[]{:S(2)}) collective-permute-start(bf16[1024,512]{1,0:T(8,128)(2,1)} %copy.29), channel_id=1, source_target_pairs={{0,1},{1,2},{2,3},{3,4},{4,5},{5,6},{6,7},{7,8},{8,9},{9,10},{10,1... | collective-permute-start | bytes 3145736 | tf_op jit(solution)/shard_map/while/body/eval_jaxpr/ppermute | solution.py:48
  759.6 40.3 %collective-permute-start.2 = (f32[1024,512]{1,0:T(8,128)}, f32[1024,512]{1,0:T(8,128)}, u32[]{:S(2)}, u32[]{:S(2)}) collective-permute-start(f32[1024,512]{1,0:T(8,128)} %convolution_add_fusion.3), channel_id=1, source_target_pairs={{0,1},{1,2},{2,3},{3,4},{4,5},{5,6},{6,7},{7,8},{8,9},{9,10},{10,1... | collective-permute-start | bytes 6291464 | tf_op jit(solution)/shard_map/while/body/eval_jaxpr/ppermute | solution.py:48
  815.0 40.3 %collective-permute-start.2 = (f32[1024,512]{1,0:T(8,128)}, f32[1024,512]{1,0:T(8,128)}, u32[]{:S(2)}, u32[]{:S(2)}) collective-permute-start(f32[1024,512]{1,0:T(8,128)} %convolution_add_fusion.3), channel_id=1, source_target_pairs={{0,1},{1,2},{2,3},{3,4},{4,5},{5,6},{6,7},{7,8},{8,9},{9,10},{10,1... | collective-permute-start | bytes 6291464 | tf_op jit(solution)/shard_map/while/body/eval_jaxpr/ppermute | solution.py:48
  870.4 40.3 %collective-permute-start.2 = (f32[1024,512]{1,0:T(8,128)}, f32[1024,512]{1,0:T(8,128)}, u32[]{:S(2)}, u32[]{:S(2)}) collective-permute-start(f32[1024,512]{1,0:T(8,128)} %convolution_add_fusion.3), channel_id=1, source_target_pairs={{0,1},{1,2},{2,3},{3,4},{4,5},{5,6},{6,7},{7,8},{8,9},{9,10},{10,1... | collective-permute-start | bytes 6291464 | tf_op jit(solution)/shard_map/while/body/eval_jaxpr/ppermute | solution.py:48
  925.8 40.3 %collective-permute-start.2 = (f32[1024,512]{1,0:T(8,128)}, f32[1024,512]{1,0:T(8,128)}, u32[]{:S(2)}, u32[]{:S(2)}) collective-permute-start(f32[1024,512]{1,0:T(8,128)} %convolution_add_fusion.3), channel_id=1, source_target_pairs={{0,1},{1,2},{2,3},{3,4},{4,5},{5,6},{6,7},{7,8},{8,9},{9,10},{10,1... | collective-permute-start | bytes 6291464 | tf_op jit(solution)/shard_map/while/body/eval_jaxpr/ppermute | solution.py:48
  981.2 40.3 %collective-permute-start.2 = (f32[1024,512]{1,0:T(8,128)}, f32[1024,512]{1,0:T(8,128)}, u32[]{:S(2)}, u32[]{:S(2)}) collective-permute-start(f32[1024,512]{1,0:T(8,128)} %convolution_add_fusion.3), channel_id=1, source_target_pairs={{0,1},{1,2},{2,3},{3,4},{4,5},{5,6},{6,7},{7,8},{8,9},{9,10},{10,1... | collective-permute-start | bytes 6291464 | tf_op jit(solution)/shard_map/while/body/eval_jaxpr/ppermute | solution.py:48
  981.2 40.3 %collective-permute-start = (bf16[1024,512]{1,0:T(8,128)(2,1)}, bf16[1024,512]{1,0:T(8,128)(2,1)S(1)}, u32[]{:S(2)}, u32[]{:S(2)}) collective-permute-start(bf16[1024,512]{1,0:T(8,128)(2,1)} %copy.29), channel_id=1, source_target_pairs={{0,1},{1,2},{2,3},{3,4},{4,5},{5,6},{6,7},{7,8},{8,9},{9,10},{10,1... | collective-permute-start | bytes 3145736 | tf_op jit(solution)/shard_map/while/body/eval_jaxpr/ppermute | solution.py:48
  1036.6 40.3 %collective-permute-start.2 = (f32[1024,512]{1,0:T(8,128)}, f32[1024,512]{1,0:T(8,128)}, u32[]{:S(2)}, u32[]{:S(2)}) collective-permute-start(f32[1024,512]{1,0:T(8,128)} %convolution_add_fusion.3), channel_id=1, source_target_pairs={{0,1},{1,2},{2,3},{3,4},{4,5},{5,6},{6,7},{7,8},{8,9},{9,10},{10,1... | collective-permute-start | bytes 6291464 | tf_op jit(solution)/shard_map/while/body/eval_jaxpr/ppermute | solution.py:48
  1092.0 40.3 %collective-permute-start.2 = (f32[1024,512]{1,0:T(8,128)}, f32[1024,512]{1,0:T(8,128)}, u32[]{:S(2)}, u32[]{:S(2)}) collective-permute-start(f32[1024,512]{1,0:T(8,128)} %convolution_add_fusion.3), channel_id=1, source_target_pairs={{0,1},{1,2},{2,3},{3,4},{4,5},{5,6},{6,7},{7,8},{8,9},{9,10},{10,1... | collective-permute-start | bytes 6291464 | tf_op jit(solution)/shard_map/while/body/eval_jaxpr/ppermute | solution.py:48
  1147.4 40.3 %collective-permute-start.2 = (f32[1024,512]{1,0:T(8,128)}, f32[1024,512]{1,0:T(8,128)}, u32[]{:S(2)}, u32[]{:S(2)}) collective-permute-start(f32[1024,512]{1,0:T(8,128)} %convolution_add_fusion.3), channel_id=1, source_target_pairs={{0,1},{1,2},{2,3},{3,4},{4,5},{5,6},{6,7},{7,8},{8,9},{9,10},{10,1... | collective-permute-start | bytes 6291464 | tf_op jit(solution)/shard_map/while/body/eval_jaxpr/ppermute | solution.py:48
  1202.8 40.3 %collective-permute-start.2 = (f32[1024,512]{1,0:T(8,128)}, f32[1024,512]{1,0:T(8,128)}, u32[]{:S(2)}, u32[]{:S(2)}) collective-permute-start(f32[1024,512]{1,0:T(8,128)} %convolution_add_fusion.3), channel_id=1, source_target_pairs={{0,1},{1,2},{2,3},{3,4},{4,5},{5,6},{6,7},{7,8},{8,9},{9,10},{10,1... | collective-permute-start | bytes 6291464 | tf_op jit(solution)/shard_map/while/body/eval_jaxpr/ppermute | solution.py:48
  1258.2 40.3 %collective-permute-start.2 = (f32[1024,512]{1,0:T(8,128)}, f32[1024,512]{1,0:T(8,128)}, u32[]{:S(2)}, u32[]{:S(2)}) collective-permute-start(f32[1024,512]{1,0:T(8,128)} %convolution_add_fusion.3), channel_id=1, source_target_pairs={{0,1},{1,2},{2,3},{3,4},{4,5},{5,6},{6,7},{7,8},{8,9},{9,10},{10,1... | collective-permute-start | bytes 6291464 | tf_op jit(solution)/shard_map/while/body/eval_jaxpr/ppermute | solution.py:48
  1258.2 40.3 %collective-permute-start = (bf16[1024,512]{1,0:T(8,128)(2,1)}, bf16[1024,512]{1,0:T(8,128)(2,1)S(1)}, u32[]{:S(2)}, u32[]{:S(2)}) collective-permute-start(bf16[1024,512]{1,0:T(8,128)(2,1)} %copy.29), channel_id=1, source_target_pairs={{0,1},{1,2},{2,3},{3,4},{4,5},{5,6},{6,7},{7,8},{8,9},{9,10},{10,1... | collective-permute-start | bytes 3145736 | tf_op jit(solution)/shard_map/while/body/eval_jaxpr/ppermute | solution.py:48
  1313.6 40.3 %collective-permute-start.2 = (f32[1024,512]{1,0:T(8,128)}, f32[1024,512]{1,0:T(8,128)}, u32[]{:S(2)}, u32[]{:S(2)}) collective-permute-start(f32[1024,512]{1,0:T(8,128)} %convolution_add_fusion.3), channel_id=1, source_target_pairs={{0,1},{1,2},{2,3},{3,4},{4,5},{5,6},{6,7},{7,8},{8,9},{9,10},{10,1... | collective-permute-start | bytes 6291464 | tf_op jit(solution)/shard_map/while/body/eval_jaxpr/ppermute | solution.py:48
  1369.0 40.3 %collective-permute-start.2 = (f32[1024,512]{1,0:T(8,128)}, f32[1024,512]{1,0:T(8,128)}, u32[]{:S(2)}, u32[]{:S(2)}) collective-permute-start(f32[1024,512]{1,0:T(8,128)} %convolution_add_fusion.3), channel_id=1, source_target_pairs={{0,1},{1,2},{2,3},{3,4},{4,5},{5,6},{6,7},{7,8},{8,9},{9,10},{10,1... | collective-permute-start | bytes 6291464 | tf_op jit(solution)/shard_map/while/body/eval_jaxpr/ppermute | solution.py:48
  1424.4 40.3 %collective-permute-start.2 = (f32[1024,512]{1,0:T(8,128)}, f32[1024,512]{1,0:T(8,128)}, u32[]{:S(2)}, u32[]{:S(2)}) collective-permute-start(f32[1024,512]{1,0:T(8,128)} %convolution_add_fusion.3), channel_id=1, source_target_pairs={{0,1},{1,2},{2,3},{3,4},{4,5},{5,6},{6,7},{7,8},{8,9},{9,10},{10,1... | collective-permute-start | bytes 6291464 | tf_op jit(solution)/shard_map/while/body/eval_jaxpr/ppermute | solution.py:48
  1479.8 40.3 %collective-permute-start.2 = (f32[1024,512]{1,0:T(8,128)}, f32[1024,512]{1,0:T(8,128)}, u32[]{:S(2)}, u32[]{:S(2)}) collective-permute-start(f32[1024,512]{1,0:T(8,128)} %convolution_add_fusion.3), channel_id=1, source_target_pairs={{0,1},{1,2},{2,3},{3,4},{4,5},{5,6},{6,7},{7,8},{8,9},{9,10},{10,1... | collective-permute-start | bytes 6291464 | tf_op jit(solution)/shard_map/while/body/eval_jaxpr/ppermute | solution.py:48
  1535.2 40.3 %collective-permute-start.2 = (f32[1024,512]{1,0:T(8,128)}, f32[1024,512]{1,0:T(8,128)}, u32[]{:S(2)}, u32[]{:S(2)}) collective-permute-start(f32[1024,512]{1,0:T(8,128)} %convolution_add_fusion.3), channel_id=1, source_target_pairs={{0,1},{1,2},{2,3},{3,4},{4,5},{5,6},{6,7},{7,8},{8,9},{9,10},{10,1... | collective-permute-start | bytes 6291464 | tf_op jit(solution)/shard_map/while/body/eval_jaxpr/ppermute | solution.py:48
  1535.2 40.3 %collective-permute-start = (bf16[1024,512]{1,0:T(8,128)(2,1)}, bf16[1024,512]{1,0:T(8,128)(2,1)S(1)}, u32[]{:S(2)}, u32[]{:S(2)}) collective-permute-start(bf16[1024,512]{1,0:T(8,128)(2,1)} %copy.29), channel_id=1, source_target_pairs={{0,1},{1,2},{2,3},{3,4},{4,5},{5,6},{6,7},{7,8},{8,9},{9,10},{10,1... | collective-permute-start | bytes 3145736 | tf_op jit(solution)/shard_map/while/body/eval_jaxpr/ppermute | solution.py:48
  1590.6 40.3 %collective-permute-start.2 = (f32[1024,512]{1,0:T(8,128)}, f32[1024,512]{1,0:T(8,128)}, u32[]{:S(2)}, u32[]{:S(2)}) collective-permute-start(f32[1024,512]{1,0:T(8,128)} %convolution_add_fusion.3), channel_id=1, source_target_pairs={{0,1},{1,2},{2,3},{3,4},{4,5},{5,6},{6,7},{7,8},{8,9},{9,10},{10,1... | collective-permute-start | bytes 6291464 | tf_op jit(solution)/shard_map/while/body/eval_jaxpr/ppermute | solution.py:48
  1645.9 40.3 %collective-permute-start.2 = (f32[1024,512]{1,0:T(8,128)}, f32[1024,512]{1,0:T(8,128)}, u32[]{:S(2)}, u32[]{:S(2)}) collective-permute-start(f32[1024,512]{1,0:T(8,128)} %convolution_add_fusion.3), channel_id=1, source_target_pairs={{0,1},{1,2},{2,3},{3,4},{4,5},{5,6},{6,7},{7,8},{8,9},{9,10},{10,1... | collective-permute-start | bytes 6291464 | tf_op jit(solution)/shard_map/while/body/eval_jaxpr/ppermute | solution.py:48
  1701.3 40.3 %collective-permute-start.2 = (f32[1024,512]{1,0:T(8,128)}, f32[1024,512]{1,0:T(8,128)}, u32[]{:S(2)}, u32[]{:S(2)}) collective-permute-start(f32[1024,512]{1,0:T(8,128)} %convolution_add_fusion.3), channel_id=1, source_target_pairs={{0,1},{1,2},{2,3},{3,4},{4,5},{5,6},{6,7},{7,8},{8,9},{9,10},{10,1... | collective-permute-start | bytes 6291464 | tf_op jit(solution)/shard_map/while/body/eval_jaxpr/ppermute | solution.py:48
  (126 other events, 2196.3 us)
Sparse Core Ops, SparseCore 0:
  1789.0 132.0 all-reduce.3
where the time goes:
time: 1940 us; the launch traced here: 1930 us
  waiting for transfers between devices  1140 us (59%)
  matrix products  597 us (31%)
  local copies, waits for them, and re-layouts  69.4 us (4%)
  loops' own time  61.4 us (3%)
  blocking collectives  37.2 us (2%)
  between operations  21.1 us (1%)
    ppermute x93, waiting for transfers between devices, visit_block(): lax.ppermute((txt_blk, ids_blk, acc_txt + part_txt), 'data', next_perm)  1030 us
    dot_general x32, matrix products, tile_terms(): lax.dot_general(emb_img, emb_txt, CONTRACT_COLS, preferred_element_type=j...  270 us
    dot_general x32, matrix products, tile_terms(): part_img = jnp.dot(grad_bf, emb_txt, preferred_element_type=jnp.float32)  162 us
    dot_general x32, matrix products, tile_terms(): lax.dot_general(grad_bf, emb_img, CONTRACT_ROWS, preferred_element_type=j...  157 us
    psum x1, waiting for transfers between devices, local_fn(): lax.psum((loss_sum + loss_part, temp_sum + temp_part, bias_sum + bias_par...  91.7 us
    another operation x1, loops' own time, local_fn(): loop_state = lax.fori_loop(0, n_dev - 1, visit_block, loop_state)  61.4 us
    while x186, local copies, waits for them, and re-layouts  49.8 us
  transfers between devices with their start and end apart: 95, of which 33 were waited for; matrix products, arithmetic and copies ran while one was open for 9% of the time, Pallas kernels for 0%

commit v1 on v0

v1 whole, which is shorter than its diff:
```python
import jax
import jax.numpy as jnp
from jax import lax
from jax.experimental import pallas as pl
from jax.experimental.pallas import tpu as pltpu
from jax.sharding import Mesh, PartitionSpec as P

CONTRACT_ROWS = (((0,), (0,)), ((), ()))
LOG2E = 1.4426950408889634
LN2 = 0.6931471805599453
ROWS_TILE = 512
COLS_TILE = 1024
COLS_SUB = 256
LANES = 128


def pair_patch(sim, ids_img, ids_txt, scale2, bias2):
    sign = jnp.where(ids_img == ids_txt, -1.0, 1.0)
    return (sim * scale2 + bias2) * sign, sign


def pair_kernel(n_rows, n_steps, scal_ref, img_ref, img_t_ref, txt_ref, txt_t_ref, idi_ref, idt_ref,
                dimg_ref, dtxt_ref, sums_ref, grad_even, grad_odd):
    step = pl.program_id(0)
    prev = jnp.maximum(step - 1, 0)

    @pl.when(step == 0)
    def _():
        grad_odd[...] = jnp.zeros_like(grad_odd)
        dimg_ref[...] = jnp.zeros_like(dimg_ref)
        sums_ref[...] = jnp.zeros_like(sums_ref)

    @pl.when(lax.rem(prev, n_rows) == 0)
    def _():
        dtxt_ref[...] = jnp.zeros_like(dtxt_ref)

    row_now = pl.multiple_of(lax.rem(jnp.minimum(step, n_steps - 1), n_rows) * ROWS_TILE, ROWS_TILE)
    row_prev = pl.multiple_of(lax.rem(prev, n_rows) * ROWS_TILE, ROWS_TILE)
    scale2 = scal_ref[0]
    bias2 = scal_ref[1]
    n_sub = COLS_TILE // COLS_SUB
    per_sub = COLS_SUB // LANES

    def similarity(sub):
        return jnp.dot(img_ref[pl.ds(row_now, ROWS_TILE), :], txt_t_ref[:, sub * COLS_SUB:(sub + 1) * COLS_SUB],
                       preferred_element_type=jnp.float32)

    def again(grad_now):
        def rows_again(piece, _):
            base = pl.multiple_of(row_now + piece * 64, 64)
            rows = pl.ds(pl.multiple_of(piece * 64, 64), 64)
            for block in range(COLS_TILE // LANES):
                cols = slice(block * LANES, block * LANES + LANES)
                sim = jnp.dot(img_ref[pl.ds(base, 64), :], txt_t_ref[:, cols], preferred_element_type=jnp.float32)
                margin, sign = pair_patch(sim, idi_ref[pl.ds(base, 64), :], idt_ref[0:1, cols], scale2, bias2)
                tail = jnp.exp2(-jnp.abs(margin))
                denom = 1.0 + tail
                grad = jnp.where(margin >= 0.0, 1.0, tail) * (1.0 / denom) * sign
                loss = LN2 * jnp.maximum(margin, 0.0) + jnp.log1p(tail)
                for index, term in enumerate((loss, grad * sim, grad)):
                    sums_ref[index] += jnp.sum(term.reshape(8, 8, LANES), axis=0)
                grad_now[block, rows, :] = grad.astype(jnp.bfloat16)
            return 0

        lax.fori_loop(0, ROWS_TILE // 64, rows_again, 0)

    def tile_pair(grad_now, grad_prev):
        zero = jnp.zeros((8, LANES), jnp.float32)
        sum_log, sum_gs, sum_g, sum_top = zero, zero, zero, zero
        sim_next = similarity(0)
        for sub in range(n_sub):
            cols = slice(sub * COLS_SUB, (sub + 1) * COLS_SUB)
            sim_sub = sim_next
            if sub + 1 < n_sub:
                sim_next = similarity(sub + 1)
            old = jnp.concatenate([grad_prev[sub * per_sub + k] for k in range(per_sub)], axis=1)
            dtxt_ref[:, cols] += jnp.dot(
                img_t_ref[:, pl.ds(row_prev, ROWS_TILE)], old, preferred_element_type=jnp.float32)
            piece = ROWS_TILE // n_sub
            old = jnp.concatenate(
                [grad_prev[k, sub * piece:(sub + 1) * piece, :] for k in range(COLS_TILE // LANES)], axis=1)
            dimg_ref[pl.ds(row_prev + sub * piece, piece), :] += jnp.dot(
                old, txt_ref[...], preferred_element_type=jnp.float32)
            for row in range(0, ROWS_TILE, 16):
                for lane in range(per_sub):
                    lane0 = lane * LANES
                    idt = idt_ref[:, sub * COLS_SUB + lane0:sub * COLS_SUB + lane0 + LANES]
                    pair = []
                    for line in (row, row + 8):
                        sim = sim_sub[line:line + 8, lane0:lane0 + LANES]
                        margin, sign = pair_patch(sim, idi_ref[pl.ds(row_now + line, 8), :], idt, scale2, bias2)
                        growth = jnp.exp2(margin)
                        denom = 1.0 + growth
                        grad = growth * (1.0 / denom) * sign
                        sum_gs = sum_gs + grad * sim
                        sum_g = sum_g + grad
                        if row % 64 == 0 and line == row:
                            if lane == 0:
                                chains = [None] * per_sub
                            chains[lane] = growth
                        else:
                            chains[lane] = growth + chains[lane] * denom
                        pair.append(grad)
                    grad_now[sub * per_sub + lane, row:row + 16, :] = jnp.concatenate(pair, axis=0).astype(jnp.bfloat16)
                if row % 64 == 48:
                    for prod in chains:
                        sum_log = sum_log + jnp.log1p(prod)
                        sum_top = sum_top + prod

        live = step < n_steps
        fits = jnp.sum(sum_top) < 1e30

        @pl.when(jnp.logical_and(live, fits))
        def _():
            sums_ref[0] += sum_log
            sums_ref[1] += sum_gs
            sums_ref[2] += sum_g

        @pl.when(jnp.logical_and(live, jnp.logical_not(fits)))
        def _():
            again(grad_now)

    @pl.when(lax.rem(step, 2) == 0)
    def _():
        tile_pair(grad_even, grad_odd)

    @pl.when(lax.rem(step, 2) == 1)
    def _():
        tile_pair(grad_odd, grad_even)


def pair_call(scal, img, img_t, txt, txt_t, idi, idt):
    n_img, width = img.shape
    n_txt = txt.shape[0]
    n_rows = n_img // ROWS_TILE
    n_cols = n_txt // COLS_TILE
    n_steps = n_rows * n_cols
    once = pl.Buffered(1)

    def col_now(step):
        return jnp.minimum(step, n_steps - 1) // n_rows

    def col_prev(step):
        return jnp.maximum(step - 1, 0) // n_rows

    return pl.pallas_call(
        lambda *refs: pair_kernel(n_rows, n_steps, *refs),
        grid=(n_steps + 1,),
        in_specs=[
            pl.BlockSpec(memory_space=pltpu.SMEM),
            pl.BlockSpec((n_img, width), lambda s: (0, 0), pipeline_mode=once),
            pl.BlockSpec((width, n_img), lambda s: (0, 0), pipeline_mode=once),
            pl.BlockSpec((COLS_TILE, width), lambda s: (col_prev(s), 0)),
            pl.BlockSpec((width, COLS_TILE), lambda s: (0, col_now(s))),
            pl.BlockSpec((n_img, LANES), lambda s: (0, 0), pipeline_mode=once),
            pl.BlockSpec((8, COLS_TILE), lambda s: (0, col_now(s))),
        ],
        out_specs=[
            pl.BlockSpec((n_img, width), lambda s: (0, 0)),
            pl.BlockSpec((width, COLS_TILE), lambda s: (0, col_prev(s))),
            pl.BlockSpec((3, 8, LANES), lambda s: (0, 0, 0)),
        ],
        out_shape=[
            jax.ShapeDtypeStruct((n_img, width), jnp.float32),
            jax.ShapeDtypeStruct((width, n_txt), jnp.float32),
            jax.ShapeDtypeStruct((3, 8, LANES), jnp.float32),
        ],
        scratch_shapes=[pltpu.VMEM((COLS_TILE // LANES, ROWS_TILE, LANES), jnp.bfloat16)] * 2,
        compiler_params=pltpu.CompilerParams(
            dimension_semantics=("arbitrary",), vmem_limit_bytes=60 * 1024 * 1024),
        cost_estimate=pl.CostEstimate(
            flops=6 * n_img * n_txt * width, bytes_accessed=4 * (n_img + n_txt) * width * 2,
            transcendentals=2 * n_img * n_txt),
        name="pair_tiles",
    )(scal, img, img_t, txt, txt_t, idi, idt)


def embed_rows(feat_rows, weights):
    raw_emb = jnp.dot(feat_rows, weights, preferred_element_type=jnp.float32)
    inv_norm = lax.rsqrt(jnp.sum(raw_emb * raw_emb, axis=1, keepdims=True))
    unit_emb = raw_emb * inv_norm
    return unit_emb, inv_norm, unit_emb.astype(jnp.bfloat16)


def weight_grad(feat_rows, unit_emb, inv_norm, grad_emb):
    raw_grad = inv_norm * (grad_emb - unit_emb * jnp.sum(unit_emb * grad_emb, axis=1, keepdims=True))
    high = lax.reduce_precision(raw_grad, 8, 7)
    low = (raw_grad - high).astype(jnp.bfloat16)
    out = lax.dot_general(feat_rows, high.astype(jnp.bfloat16), CONTRACT_ROWS, preferred_element_type=jnp.float32)
    return out + lax.dot_general(feat_rows, low, CONTRACT_ROWS, preferred_element_type=jnp.float32)


def solution(mesh):
    n_dev = mesh.shape["data"]
    n_z = 4
    n_p = n_dev // n_z
    grid_mesh = Mesh(mesh.devices.reshape(n_z, n_p), ("z", "p"))
    rows = P(("z", "p"))

    def local_fn(feat_img, feat_txt, w_img, w_txt, log_temp, logit_bias, pair_ids):
        total_rows = feat_img.shape[0] * n_dev
        temp_scale = jnp.exp(log_temp)
        ids_all = lax.all_gather(pair_ids, ("z", "p"), tiled=True).reshape(n_z, n_p, -1)
        ids_img = lax.dynamic_index_in_dim(ids_all, lax.axis_index("p"), 1, keepdims=False).reshape(-1)
        ids_txt = lax.dynamic_index_in_dim(ids_all, lax.axis_index("z"), 0, keepdims=False).reshape(-1)
        feat_img = lax.all_gather(feat_img, "z", tiled=True)
        feat_txt = lax.all_gather(feat_txt, "p", tiled=True)
        unit_img, inv_img, emb_img = embed_rows(feat_img, w_img)
        unit_txt, inv_txt, emb_txt = embed_rows(feat_txt, w_txt)
        scal = jnp.stack([temp_scale * LOG2E, logit_bias * LOG2E])
        idi = jnp.broadcast_to(ids_img[:, None], (ids_img.shape[0], LANES))
        idt = jnp.broadcast_to(ids_txt[None, :], (8, ids_txt.shape[0]))
        part_img, part_txt_t, sums = pair_call(scal, emb_img, emb_img.T, emb_txt, emb_txt.T, idi, idt)
        step_scale = temp_scale / total_rows
        dw_img = weight_grad(feat_img, unit_img, inv_img, step_scale * part_img)
        dw_txt = weight_grad(feat_txt, unit_txt, inv_txt, step_scale * part_txt_t.T)
        sums = jnp.sum(sums, axis=(1, 2)) / total_rows
        sums, dw_img, dw_txt = lax.psum((sums, dw_img, dw_txt), ("z", "p"))
        return sums[0], temp_scale * sums[1], sums[2], dw_img, dw_txt

    return jax.shard_map(
        local_fn,
        mesh=grid_mesh,
        in_specs=(P(("z", "p"), None), P(("z", "p"), None), P(None, None), P(None, None), P(), P(), rows),
        out_specs=(P(), P(), P(), P(None, None), P(None, None)),
        check_vma=False,
    )
```

time: 1940 us -> 643 us (0.33)
  waiting for transfers between devices: 1140 us -> 199 us
  matrix products: 597 us -> 74 us
  Pallas kernels: 0 us -> 182 us
  loops' own time: 61.4 us -> 0 us
  blocking collectives: 37.2 us -> 84 us
  other arithmetic: 4.4 us -> 40.8 us
  local copies, waits for them, and re-layouts: 69.4 us -> 45.9 us
    ppermute x94 -> x0, waiting for transfers between devices: 1050 us -> none  [the longest x93 1030 us: visit_block(): lax.ppermute((txt_blk, ids_blk, acc_txt + part_txt), 'data', next_perm)]
    dot_general x98 -> x4, matrix products: 594 us -> 56.7 us  [the longest x2 28.4 us: weight_grad(): lax.dot_general(feat_rows, low, CONTRACT_ROWS, preferred_element_type=jnp...]
    pallas_call x0 -> x1, Pallas kernels: none -> 182 us  [pair_call(): pl.pallas_call(lambda *refs: pair_kernel(n_rows, n_steps, *refs), grid=(n...]
    all_gather x0 -> x2, waiting for transfers between devices: none -> 102 us  [the longest x1 72.6 us: local_fn(): feat_img = lax.all_gather(feat_img, 'z', tiled=True)]
    another operation x1 -> x0, loops' own time: 61.4 us -> none  [local_fn(): loop_state = lax.fori_loop(0, n_dev - 1, visit_block, loop_state)]
    while x188 -> x0, local copies, waits for them, and re-layouts: 55.6 us -> none
    all_gather x0 -> x1, blocking collectives: none -> 44.2 us  [local_fn(): lax.all_gather(pair_ids, ('z', 'p'), tiled=True).reshape(n_z, n_p, -1)]
    convert_element_type x2 -> x4, other arithmetic: 2.45 us -> 23.3 us  [embed_rows(): return (unit_emb, inv_norm, unit_emb.astype(jnp.bfloat16))]
  transfers between devices with their start and end apart: 95 -> 3, of which waited for: 33 -> 3; matrix products, arithmetic and copies ran while one was open for 9% -> 4% of each run, Pallas kernels for 0% -> 0%
where the time goes in v1:
time: 643 us; the launch traced here: 642 us
  waiting for transfers between devices  199 us (31%)
  Pallas kernels  182 us (28%)
  blocking collectives  84 us (13%)
  matrix products  74 us (12%)
  local copies, waits for them, and re-layouts  45.9 us (7%)
  other arithmetic  40.8 us (6%)
  between operations  17 us (3%)
    pallas_call x1, Pallas kernels, pair_call(): pl.pallas_call(lambda *refs: pair_kernel(n_rows, n_steps, *refs), grid=(n...  182 us
    psum x1, waiting for transfers between devices, local_fn(): sums, dw_img, dw_txt = lax.psum((sums, dw_img, dw_txt), ('z', 'p'))  95.2 us
    all_gather x1, waiting for transfers between devices, local_fn(): feat_img = lax.all_gather(feat_img, 'z', tiled=True)  72.6 us
    all_gather x1, blocking collectives, local_fn(): lax.all_gather(pair_ids, ('z', 'p'), tiled=True).reshape(n_z, n_p, -1)  44.2 us
    psum x1, blocking collectives, local_fn(): sums, dw_img, dw_txt = lax.psum((sums, dw_img, dw_txt), ('z', 'p'))  39.9 us
    all_gather x1, waiting for transfers between devices, local_fn(): feat_txt = lax.all_gather(feat_txt, 'p', tiled=True)  29.5 us
    dot_general x2, matrix products, weight_grad(): lax.dot_general(feat_rows, low, CONTRACT_ROWS, preferred_element_type=jnp...  28.4 us
    dot_general x2, matrix products, weight_grad(): lax.dot_general(feat_rows, high.astype(jnp.bfloat16), CONTRACT_ROWS, pref...  28.3 us
  transfers between devices with their start and end apart: 3, of which 3 were waited for; matrix products, arithmetic and copies ran while one was open for 4% of the time, Pallas kernels for 0%

profile of v1, /device:TPU:0, one launch (start us, length us, event | category | flops | bytes accessed | tf_op | source)
XLA Modules:
  0.0 642.2 jit_solution(1652612935587863338)
XLA Ops:
  7.2 0.0 copy-start
  7.2 0.0 all-gather.3.cloned.1.call-start
  7.2 0.7 all-gather.3.cloned.1.call-update
  7.9 0.0 all-gather.5.cloned.1.call-start
  8.0 0.7 all-gather.5.cloned.1.call-update
  8.7 0.0 all-reduce.3.cloned.1.call-start
  8.7 44.2 %all_gather.11 = s32[32768]{0:T(1024)S(1)} all-gather(s32[1024]{0:T(1024)} %param.13), channel_id=1, replica_groups=mesh['z'=4,'p'=8] {'z','p'}, dimensions={0}, use_global_device_ids=true | all-gather | bytes 135168 | tf_op jit(solution)/shard_map/all_gather | solution.py:203
  54.3 0.6 pad_maximum_fusion.refs_0_
  54.9 72.6 %all-gather.3.cloned.1.call-done = bf16[4096,768]{1,0:T(8,128)(2,1)} async-done(((bf16[1024,768]{1,0:T(8,128)(2,1)}), bf16[4096,768]{1,0:T(8,128)(2,1)}) %all-gather.3.cloned.1.call-update) | async-done | bytes 6291472 | tf_op jit(solution)/shard_map/all_gather | solution.py:206
  127.5 0.0 copy-done
  127.5 5.8 multiply_reduce_fusion.2
  133.3 0.0 copy-start.3
  133.3 3.2 copy-done.3
  136.5 3.0 multiply_convert_fusion.1
  139.6 6.5 %copy.17.refs_1_ = bf16[4096,512]{1,0:T(8,128)(2,1)} copy(bf16[4096,512]{0,1:T(8,128)(2,1)} %multiply_convert_fusion.1) | data formatting | bytes 8388608 | tf_op jit(solution)/shard_map/convert_element_type | solution.py:182
  146.0 0.0 copy-start.5
  146.0 6.5 %fusion.28.refs_2_ = bf16[512,4096]{1,0:T(8,128)(2,1)} fusion(f32[4096,512]{0,1:T(8,128)} %copy-done.3, f32[4096]{0:T(1024)S(1)} %rsqrt.16), kind=kLoop, calls=%fused_computation.30 | loop fusion | flops 4194304 | bytes 12599296 | tf_op jit(solution)/shard_map/convert_element_type | solution.py:182
  152.5 29.5 %all-gather.5.cloned.1.call-done = bf16[8192,512]{1,0:T(8,128)(2,1)} async-done(((bf16[1024,512]{1,0:T(8,128)(2,1)}), bf16[8192,512]{1,0:T(8,128)(2,1)}) %all-gather.5.cloned.1.call-update) | async-done | bytes 8388624 | tf_op jit(solution)/shard_map/all_gather | solution.py:207
  182.0 0.0 copy-done.5
  182.0 11.5 %multiply_reduce_fusion = (f32[8192]{0:T(1024)S(1)}, f32[8192,512]{0,1:T(8,128)}) fusion(bf16[8192,512]{1,0:T(8,128)(2,1)} %all-gather.5.cloned.1.call-done, bf16[512,512]{1,0:T(8,128)(2,1)S(1)} %copy-done.5), kind=kOutput, calls=%fused_computation.7 | convolution fusion | flops 4303347712 | bytes 25722880 | tf_op jit(solution)/shard_map/dot_general | solution.py:179
  193.5 0.0 copy-start.2
  193.5 9.5 %multiply_convert_fusion = bf16[8192,512]{0,1:T(8,128)(2,1)} fusion(f32[8192,512]{0,1:T(8,128)} %get-tuple-element.29, f32[8192]{0:T(1024)S(1)} %rsqrt.17), kind=kLoop, calls=%fused_computation.8 | loop fusion | flops 8388608 | bytes 25198592 | tf_op jit(solution)/shard_map/convert_element_type | solution.py:182
  203.1 4.1 copy-done.2
  207.2 4.2 fusion.27.refs_4_
  211.4 11.9 %copy.18.refs_3_ = bf16[8192,512]{1,0:T(8,128)(2,1)} copy(bf16[8192,512]{0,1:T(8,128)(2,1)} %multiply_convert_fusion) | data formatting | bytes 16777216 | tf_op jit(solution)/shard_map/convert_element_type | solution.py:182
  223.3 2.9 broadcast_in_dim.9.refs_5_
  226.3 0.7 broadcast_in_dim.21.refs_6_
  227.0 181.6 %pair_tiles.1 = (f32[4096,512]{1,0:T(8,128)}, f32[512,8192]{1,0:T(8,128)}, f32[3,8,128]{2,1,0:T(8,128)}) custom-call(f32[2]{0:T(128)} %pad_maximum_fusion.refs_0_, bf16[4096,512]{1,0:T(8,128)(2,1)} %copy.17.refs_1_, bf16[512,4096]{1,0:T(8,128)(2,1)} %fusion.28.refs_2_, bf16[8192,512]{1,0:T(8,128)(2,1)} %copy.18.refs_3_, bf16[512,8192]{1,0:T(8,128)(2,1)} %fusion.27.refs_4_, ...), custom_call_target="tpu_custom_call" | custom-call | flops 103079215104 | bytes 50331648 | tf_op jit(solution)/shard_map/pair_tiles/pallas_call | solution.py:146
  408.6 8.9 %copy.19 = f32[4096,512]{0,1:T(8,128)} copy(f32[4096,512]{1,0:T(8,128)} %get-tuple-element.9) | data formatting | bytes 16777216 | tf_op jit(solution)/shard_map/pair_tiles/pallas_call | solution.py:146
  417.5 0.0 copy-start.4
  417.5 11.6 %fusion.1 = f32[8192]{0:T(1024)S(1)} fusion(f32[512,8192]{1,0:T(8,128)} %get-tuple-element.10, f32[8192,512]{0,1:T(8,128)} %get-tuple-element.29, f32[]{:T(128)S(6)} %div.7, f32[8192]{0:T(1024)S(1)} %rsqrt.17), kind=kLoop, calls=%fused_computation.5 | loop fusion | flops 16769024 | bytes 33619972 | tf_op jit(solution)/shard_map/reduce_sum | solution.py:186
  429.2 1.4 copy-done.4
  430.5 5.2 multiply_reduce_fusion.1
  435.8 15.5 %fusion.6 = f32[512,512]{1,0:T(8,128)S(1)} fusion(bf16[8192,512]{1,0:T(8,128)(2,1)} %all-gather.5.cloned.1.call-done, f32[512,8192]{1,0:T(8,128)} %get-tuple-element.10, f32[8192,512]{0,1:T(8,128)} %get-tuple-element.29, f32[8192]{0:T(1024)S(1)} %fusion.1, f32[]{:T(128)S(6)} %div.7, f32[8192]{0:T(1024)S(1)} %rsqrt.17), kind=kOutput, calls=%fused_computation.13 | convolution fusion | flops 4324327424 | bytes 43057156 | tf_op jit(solution)/shard_map/dot_general | solution.py:189
  451.3 18.4 %fusion.15 = f32[512,512]{0,1:T(8,128)} fusion(f32[512,512]{1,0:T(8,128)S(1)} %fusion.6, bf16[8192,512]{1,0:T(8,128)(2,1)} %all-gather.5.cloned.1.call-done, f32[8192]{0:T(1024)S(1)} %fusion.1, f32[8192,512]{0,1:T(8,128)} %get-tuple-element.29, f32[512,8192]{1,0:T(8,128)} %get-tuple-element.10, f32[]{:T(128)S(6)} %div.7, f32[8192]{0:T(1024)S(1)} %rsqrt.17), kind=kOutput, calls=%fused_computation.22 | convolution fusion | flops 4328783872 | bytes 44105732 | tf_op jit(solution)/shard_map/dot_general | solution.py:190
  469.7 10.0 %fusion.7 = f32[512,768]{1,0:T(8,128)S(1)} fusion(bf16[4096,768]{1,0:T(8,128)(2,1)} %all-gather.3.cloned.1.call-done, f32[4096,512]{0,1:T(8,128)} %copy.19, f32[4096,512]{0,1:T(8,128)} %copy-done.3, f32[4096]{0:T(1024)S(1)} %multiply_reduce_fusion.1, f32[]{:T(128)S(6)} %div.7, f32[4096]{0:T(1024)S(1)} %rsqrt.16), kind=kOutput, calls=%fused_computation.18 | convolution fusion | flops 3238002688 | bytes 24674308 | tf_op jit(solution)/shard_map/dot_general | solution.py:190
  479.7 0.0 copy-start.6
  479.7 0.0 copy-start.1
  479.7 12.7 %add_bitcast_fusion = f32[768,512]{0,1:T(8,128)} fusion(f32[512,768]{1,0:T(8,128)S(1)} %fusion.7, bf16[4096,768]{1,0:T(8,128)(2,1)} %all-gather.3.cloned.1.call-done, f32[4096]{0:T(1024)S(1)} %multiply_reduce_fusion.1, f32[4096,512]{0,1:T(8,128)} %copy-done.3, f32[4096,512]{0,1:T(8,128)} %copy.19, f32[]{:T(128)S(6)} %div.7, f32[4096]{0:T(1024)S(1)} %rsqrt.16), kind=kOutput, calls=%fused_computation.20 | convolution fusion | flops 3236298752 | bytes 26247172 | tf_op jit(solution)/shard_map/dot_general | solution.py:189
  492.5 0.0 all-reduce.3.cloned.1.call-update
  492.5 0.0 copy-done.6
  492.5 0.1 reduce_sum.47
  492.6 39.9 %psum.21 = f32[3]{0:T(128)S(1)} all-reduce(f32[3]{0:T(128)S(1)} %broadcast_multiply_fusion), channel_id=1, replica_groups=mesh['z'=4,'p'=8] {'z','p'}, use_global_device_ids=true, to_apply=%region_3.4 | all-reduce | flops 3 | bytes 24 | tf_op jit(solution)/shard_map/psum | solution.py:218
  532.5 0.6 fusion.18
  533.8 95.2 %all-reduce.3.cloned.1.call-done = (f32[768,512]{0,1:T(8,128)}, f32[512,512]{0,1:T(8,128)}) async-done(((f32[768,512]{0,1:T(8,128)}, f32[512,512]{0,1:T(8,128)}), (f32[768,512]{0,1:T(8,128)}, f32[512,512]{0,1:T(8,128)})) %all-reduce.3.cloned.1.call-update) | async-done | bytes 2621456 | tf_op jit(solution)/shard_map/psum | solution.py:218
  629.0 3.0 copy.20
  632.0 2.5 copy.21
  634.5 0.0 copy-done.1
  (7 shorter events, 0.1 us)
Async XLA Ops:
  7.2 120.4 %copy-start = (bf16[768,512]{1,0:T(8,128)(2,1)S(1)}, bf16[768,512]{1,0:T(8,128)(2,1)}, u32[]{:S(2)}) copy-start(bf16[768,512]{1,0:T(8,128)(2,1)} %param.9) | copy-start | bytes 2359300
  7.2 120.3 %all-gather.3.cloned.1.call-start = ((), (), s32[]{:S(2)}) async-start(), calls=%async_computation | async-start | bytes 7864320 | tf_op jit(solution)/shard_map/all_gather | solution.py:206
  7.9 174.1 %all-gather.5.cloned.1.call-start = ((), (), s32[]{:S(2)}) async-start(), calls=%async_computation.1 | async-start | bytes 9437184 | tf_op jit(solution)/shard_map/all_gather | solution.py:207
  8.7 620.3 %all-reduce.3.cloned.1.call-start = ((), (), s32[]{:S(2)}) async-start(), calls=%async_computation.2 | async-start | bytes 5242880 | tf_op jit(solution)/shard_map/psum | solution.py:218
  133.3 3.2 copy-start.3
  146.0 36.0 %copy-start.5 = (bf16[512,512]{1,0:T(8,128)(2,1)S(1)}, bf16[512,512]{1,0:T(8,128)(2,1)}, u32[]{:S(2)}) copy-start(bf16[512,512]{1,0:T(8,128)(2,1)} %param.10) | copy-start | bytes 1572868
  193.5 13.6 %copy-start.2 = (f32[8192,512]{0,1:T(8,128)S(1)}, f32[8192,512]{0,1:T(8,128)}, u32[]{:S(2)}) copy-start(f32[8192,512]{0,1:T(8,128)} %get-tuple-element.29) | copy-start | bytes 50331652
  417.5 13.0 %copy-start.4 = (f32[4096,512]{0,1:T(8,128)S(1)}, f32[4096,512]{0,1:T(8,128)}, u32[]{:S(2)}) copy-start(f32[4096,512]{0,1:T(8,128)} %copy.19) | copy-start | bytes 25165828
  479.7 12.8 %copy-start.6 = (f32[3,8,128]{2,1,0:T(8,128)S(1)}, f32[3,8,128]{2,1,0:T(8,128)}, u32[]{:S(2)}) copy-start(f32[3,8,128]{2,1,0:T(8,128)} %get-tuple-element.8) | copy-start | bytes 36868
  479.7 154.8 %copy-start.1 = (bf16[768,512]{1,0:T(8,128)(2,1)S(1)}, bf16[768,512]{1,0:T(8,128)(2,1)}, u32[]{:S(2)}) copy-start(bf16[768,512]{1,0:T(8,128)(2,1)} %param.9) | copy-start | bytes 2359300
Sparse Core Ops, SparseCore 0:
  9.6 117.9 all-gather.2
  129.4 52.5 all-gather.4
  492.6 136.2 all-reduce.2
